TPU v7x, 32 devices: a whole 2x2x4 slice. The times are simulated.
32 devices in a mesh: dp: 8 (over z, x), owner: 4 (over y, core).
Axes of the slice: x: 2, y: 2, z: 4, core: 2. Of those that a mesh axis runs over, the one named last changes fastest.
Arguments:
- gradients: float32 [8, 1024, 7168], P(None, 'dp', 'owner'), may hold values from -6 to 6
- rows_live: int32 [8], replicated, may hold values from 256 to 1024
Outputs:
- updates: bfloat16 [8, 1024, 7168], P(None, 'dp', 'owner')
All inputs are finite; a program needn't handle non-finite values.
Results may differ from a plain program's by a relative error of at most 0.015.
Values may be sent and summed in bfloat16 or wider, within the bound.
A program may use at most 64 MiB of HBM per device.

v0:
```python
import math
import jax
import jax.numpy as jnp
from jax import lax
from jax.sharding import PartitionSpec as P

D = 7168


def body(gradients, rows_live):
    narrowed = gradients.astype(jnp.bfloat16)
    regrouped = lax.all_to_all(narrowed, "dp", split_axis=0, concat_axis=1, tiled=True)
    owned_count = regrouped.shape[0]
    hidden_rows = regrouped.shape[1]
    first_owned = lax.axis_index("dp") * owned_count
    live_counts = lax.dynamic_slice_in_dim(rows_live, first_owned, owned_count)
    live_mask = jnp.arange(hidden_rows, dtype=jnp.int32)[None, :, None] < live_counts[:, None, None]
    regrouped = jnp.where(live_mask, regrouped, jnp.zeros_like(regrouped))
    partial_gram = jnp.einsum(
        "mcr,mdr->mcd", regrouped, regrouped, preferred_element_type=jnp.float32
    )
    live_float = live_counts.astype(jnp.float32)
    whole_gram = lax.psum(partial_gram.astype(jnp.bfloat16), "owner").astype(jnp.float32)
    trace_total = jnp.trace(whole_gram, axis1=1, axis2=2)
    scale_sq = 2.0 * trace_total / live_float
    normed_gram = (whole_gram / scale_sq[:, None, None]).astype(jnp.bfloat16)
    inverse = (1.0 / jnp.sqrt(scale_sq))[:, None, None]
    once = (
        jnp.einsum("mcd,mdr->mcr", normed_gram, regrouped, preferred_element_type=jnp.float32)
        * inverse
    )
    twice = jnp.einsum(
        "mcd,mdr->mcr", normed_gram, once.astype(jnp.bfloat16), preferred_element_type=jnp.float32
    )
    combined = 3.4445 * regrouped.astype(jnp.float32) * inverse - 4.775 * once + 2.0315 * twice
    update_rows = (combined * (0.2 * math.sqrt(D))).astype(jnp.bfloat16)
    return lax.all_to_all(update_rows, "dp", split_axis=1, concat_axis=0, tiled=True)


def solution(mesh):
    return jax.shard_map(
        body,
        mesh=mesh,
        in_specs=(P(None, "dp", "owner"), P()),
        out_specs=P(None, "dp", "owner"),
        check_vma=False,
    )
```

profile of v0, /device:TPU:0, one launch (start us, length us, event | category | flops | bytes accessed | tf_op | source)
XLA Modules:
  0.0 389.9 jit_solution(16820926485267107496)
XLA Ops:
  6.5 5.3 %convert_element_type.32 = bf16[8,128,1792]{2,1,0:T(8,128)(2,1)} convert(f32[8,128,1792]{2,1,0:T(8,128)} %param.2) | non-fusion elementwise | flops 1835008 | bytes 11010048 | tf_op jit(solution)/shard_map/convert_element_type | solution.py:11
  11.9 0.0 copy-start.2
  11.9 7.4 %all-to-all-start = ((bf16[8,128,1792]{2,1,0:T(8,128)(2,1)}), bf16[8,128,1792]{2,1,0:T(8,128)(2,1)}, u32[]{:S(2)}, u32[]{:S(2)}) async-start(bf16[8,128,1792]{2,1,0:T(8,128)(2,1)} %convert_element_type.32), calls=%async_computation | async-start | bytes 7340032 | tf_op jit(solution)/shard_map/all_to_all | solution.py:12
  19.3 0.0 all-reduce.2.cloned.1.call-start
  19.3 0.0 copy-done.2
  19.3 0.6 dynamic_slice.3
  19.9 0.6 iota_compare_fusion.1
  20.6 80.8 %all-to-all-done = bf16[8,128,1792]{2,1,0:T(8,128)(2,1)} async-done(((bf16[8,128,1792]{2,1,0:T(8,128)(2,1)}), bf16[8,128,1792]{2,1,0:T(8,128)(2,1)}, u32[]{:S(2)}, u32[]{:S(2)}) %all-to-all-start) | async-done | bytes 3670048 | tf_op jit(solution)/shard_map/all_to_all | solution.py:12
  101.3 8.6 %convert_bitcast_fusion = bf16[1,1024,1024]{2,1,0:T(8,128)(2,1)} fusion(bf16[1,1024,1,1,1,1,1792]{6,1,5,4,3,2,0:T(8,128)(2,1)} %bitcast.2, pred[1024]{0:T(1024)(128)(4,1)S(1)} %iota_compare_fusion.1), kind=kOutput, calls=%fused_computation.16 | convolution fusion | flops 3760979968 | bytes 5768192 | tf_op jit(solution)/shard_map/mcr,mdr->mcd/dot_general | solution.py:19
  109.9 0.0 all-reduce.2.cloned.1.call-update
  110.5 4.2 %bitcast_select_fusion = bf16[1024,1792]{1,0:T(8,128)(2,1)} fusion(bf16[8,128,1792]{2,1,0:T(8,128)(2,1)} %all-to-all-done, pred[1024]{0:T(1024)(128)(4,1)S(1)} %iota_compare_fusion.1), kind=kLoop, calls=%fused_computation.11 | loop fusion | flops 1835008 | bytes 7341056 | tf_op jit(solution)/shard_map/jit(_where)/select_n | solution.py:18
  114.7 45.8 %all-reduce.2.cloned.1.call-done = bf16[1,1024,1024]{2,1,0:T(8,128)(2,1)} async-done(((bf16[1,1024,1024]{2,1,0:T(8,128)(2,1)}), bf16[1,1024,1024]{2,1,0:T(8,128)(2,1)}) %all-reduce.2.cloned.1.call-update) | async-done | bytes 2097168 | tf_op jit(solution)/shard_map/psum | solution.py:23
  160.6 2.4 fusion
  163.7 0.0 copy-start
  163.8 0.0 copy-start.1
  163.8 9.9 %fusion.2 = f32[1024,1792]{1,0:T(8,128)} fusion(bf16[1,1024,1,1,1,1,1792]{6,1,5,4,3,2,0:T(8,128)(2,1)} %bitcast.2, pred[1024]{0:T(1024)(128)(4,1)S(1)} %iota_compare_fusion.1, bf16[1,1024,1024]{2,1,0:T(8,128)(2,1)} %all-reduce.2.cloned.1.call-done, f32[]{:T(128)} %bitcast.7), kind=kOutput, calls=%fused_computation.7 | convolution fusion | flops 3763077120 | bytes 13108228 | tf_op jit(solution)/shard_map/mcd,mdr->mcr/dot_general | solution.py:29
  173.6 0.0 copy-done
  173.6 0.0 copy-done.1
  173.6 10.1 %fusion.7 = bf16[1,1024,1792]{2,1,0:T(8,128)(2,1)S(1)} fusion(f32[1024,1792]{1,0:T(8,128)} %fusion.2, f32[]{:T(128)} %bitcast.6, f32[]{:T(128)S(6)} %mul.54, bf16[1024,1792]{1,0:T(8,128)(2,1)S(1)} %copy-done, bf16[1,1024,1024]{2,1,0:T(8,128)(2,1)S(1)} %copy-done.1, f32[]{:T(128)} %bitcast.7), kind=kOutput, calls=%fused_computation.14 | convolution fusion | flops 3781427200 | bytes 16777228 | tf_op jit(solution)/shard_map/mcd,mdr->mcr/dot_general | solution.py:32
  183.8 52.2 %copy.7 = bf16[1,1024,1792]{2,0,1:T(2,128)(2,1)} copy(bf16[1,1024,1792]{2,1,0:T(8,128)(2,1)S(1)} %fusion.7) | data formatting | bytes 7340032 | tf_op jit(solution)/shard_map/convert_element_type | solution.py:36
  236.0 0.6 broadcast.60
  236.6 38.7 %reduce.1 = bf16[1024,1792]{1,0:T(8,128)(2,1)} reduce(bf16[1024,1,1792]{2,1,0:T(2,128)(2,1)} %bitcast.27, bf16[]{:T(256)} %broadcast.60), dimensions={1}, to_apply=%bitcast.26.reduce_sub_computation | reduce | bytes 7340034
  275.2 6.6 %reshape.127 = bf16[8,2,114688]{2,1,0:T(2,128)(2,1)} reshape(bf16[1024,1792]{1,0:T(8,128)(2,1)} %reduce.1) | data formatting | bytes 7340032
  281.8 87.5 %all_to_all.27 = bf16[8,2,114688]{2,1,0:T(2,128)(2,1)} all-to-all(bf16[8,2,114688]{2,1,0:T(2,128)(2,1)} %reshape.127), channel_id=1, replica_groups=mesh['dp'=8,'owner'=4] {'dp'}, dimensions={0} | all-to-all | bytes 7340032 | tf_op jit(solution)/shard_map/all_to_all | solution.py:37
  369.3 8.3 %reshape.128 = bf16[1024,1,1792]{2,1,0:T(2,128)(2,1)} reshape(bf16[8,2,114688]{2,1,0:T(2,128)(2,1)} %all_to_all.27) | data formatting | bytes 7340032
  377.6 5.5 %copy.5 = bf16[1,1024,1792]{2,1,0:T(8,128)(2,1)} copy(bf16[1,1024,1792]{2,0,1:T(2,128)(2,1)} %bitcast.28) | data formatting | bytes 7340032
Async XLA Ops:
  11.9 7.5 %copy-start.2 = (s32[8]{0:T(128)S(1)}, s32[8]{0:T(128)}, u32[]{:S(2)}) copy-start(s32[8]{0:T(128)} %param.3) | copy-start | bytes 100
  11.9 89.5 %all-to-all-start = ((bf16[8,128,1792]{2,1,0:T(8,128)(2,1)}), bf16[8,128,1792]{2,1,0:T(8,128)(2,1)}, u32[]{:S(2)}, u32[]{:S(2)}) async-start(bf16[8,128,1792]{2,1,0:T(8,128)(2,1)} %convert_element_type.32), calls=%async_computation | async-start | bytes 7340032 | tf_op jit(solution)/shard_map/all_to_all | solution.py:12
  19.3 141.3 %all-reduce.2.cloned.1.call-start = ((), (), s32[]{:S(2)}) async-start(), calls=%async_computation.2 | async-start | bytes 4194304 | tf_op jit(solution)/shard_map/psum | solution.py:23
  163.7 9.9 %copy-start = (bf16[1024,1792]{1,0:T(8,128)(2,1)S(1)}, bf16[1024,1792]{1,0:T(8,128)(2,1)}, u32[]{:S(2)}) copy-start(bf16[1024,1792]{1,0:T(8,128)(2,1)} %bitcast_select_fusion) | copy-start | bytes 11010052
  163.8 9.9 %copy-start.1 = (bf16[1,1024,1024]{2,1,0:T(8,128)(2,1)S(1)}, bf16[1,1024,1024]{2,1,0:T(8,128)(2,1)}, u32[]{:S(2)}) copy-start(bf16[1,1024,1024]{2,1,0:T(8,128)(2,1)} %all-reduce.2.cloned.1.call-done) | copy-start | bytes 6291460
Sparse Core Ops, SparseCore 0:
  110.0 50.4 all-reduce.1
where the time goes:
time: 391 us; the launch traced here: 390 us
  waiting for transfers between devices  127 us (32%)
  blocking collectives  87.5 us (22%)
  local copies, waits for them, and re-layouts  73.8 us (19%)
  other arithmetic  51.2 us (13%)
  matrix products  28.5 us (7%)
  between operations  14.8 us (4%)
  starting transfers between devices  7.45 us (2%)
    all_to_all x1, blocking collectives, body(): lax.all_to_all(update_rows, 'dp', split_axis=1, concat_axis=0, tiled=True)  87.5 us
    all_to_all x1, waiting for transfers between devices, body(): lax.all_to_all(narrowed, 'dp', split_axis=0, concat_axis=1, tiled=True)  80.8 us
    convert_element_type x1, local copies, waits for them, and re-layouts, body(): update_rows = (combined * (0.2 * math.sqrt(D))).astype(jnp.bfloat16)  52.2 us
    psum x1, waiting for transfers between devices, body(): lax.psum(partial_gram.astype(jnp.bfloat16), 'owner').astype(jnp.float32)  45.8 us
    unnamed x1, other arithmetic  38.7 us
    unnamed x10, local copies, waits for them, and re-layouts  21 us
    dot_general x1, matrix products, body(): jnp.einsum('mcd,mdr->mcr', normed_gram, once.astype(jnp.bfloat16), prefer...  10.1 us
    dot_general x1, matrix products, body(): jnp.einsum('mcd,mdr->mcr', normed_gram, regrouped, preferred_element_type...  9.87 us
  transfers between devices with their start and end apart: 2, of which 2 were waited for; matrix products, arithmetic and copies ran while one was open for 1% of the time, Pallas kernels for 0%

commit v1 on v0

--- a/solution.py
+++ b/solution.py
@@ -5,6 +5,13 @@
 from jax.sharding import PartitionSpec as P
 
 D = 7168
+
+
+def stacked_exchange(value, name, split, join):
+    size = lax.axis_size(name)
+    tiles = jnp.stack(jnp.split(value, size, axis=split), axis=0)
+    tiles = lax.all_to_all(tiles, name, split_axis=0, concat_axis=0)
+    return jnp.concatenate(tiles, axis=join)
 
 
 def body(gradients, rows_live):
@@ -34,7 +41,7 @@
     )
     combined = 3.4445 * regrouped.astype(jnp.float32) * inverse - 4.775 * once + 2.0315 * twice
     update_rows = (combined * (0.2 * math.sqrt(D))).astype(jnp.bfloat16)
-    return lax.all_to_all(update_rows, "dp", split_axis=1, concat_axis=0, tiled=True)
+    return stacked_exchange(update_rows, "dp", 1, 0)
 
 
 def solution(mesh):

time: 391 us -> 280 us (0.72)
  local copies, waits for them, and re-layouts: 73.8 us -> 2.66 us
  other arithmetic: 51.2 us -> 12.5 us
    convert_element_type x1 -> x0, local copies, waits for them, and re-layouts: 52.2 us -> none  [body(): update_rows = (combined * (0.2 * math.sqrt(D))).astype(jnp.bfloat16)]
    unnamed x1 -> x0, other arithmetic: 38.7 us -> none
    unnamed x10 -> x14, local copies, waits for them, and re-layouts: 21 us -> 2.07 us
  transfers between devices with their start and end apart: 2 -> 2, of which waited for: 2 -> 2; matrix products, arithmetic and copies ran while one was open for 1% -> 2% of each run, Pallas kernels for 0% -> 0%
where the time goes in v1:
time: 280 us
  waiting for transfers between devices  127 us (45%)
  blocking collectives  87.2 us (31%)
  matrix products  28.3 us (10%)
  between operations  14.8 us (5%)
  other arithmetic  12.5 us (4%)
  starting transfers between devices  7.45 us (3%)
    all_to_all x1, blocking collectives, stacked_exchange(): tiles = lax.all_to_all(tiles, name, split_axis=0, concat_axis=0)  87.2 us
    all_to_all x1, waiting for transfers between devices, body(): lax.all_to_all(narrowed, 'dp', split_axis=0, concat_axis=1, tiled=True)  80.9 us
    psum x1, waiting for transfers between devices, body(): lax.psum(partial_gram.astype(jnp.bfloat16), 'owner').astype(jnp.float32)  45.9 us
    dot_general x1, matrix products, body(): jnp.einsum('mcd,mdr->mcr', normed_gram, once.astype(jnp.bfloat16), prefer...  9.87 us
    dot_general x1, matrix products, body(): jnp.einsum('mcd,mdr->mcr', normed_gram, regrouped, preferred_element_type...  9.86 us
    dot_general x1, matrix products, body(): jnp.einsum('mcr,mdr->mcd', regrouped, regrouped, preferred_element_type=j...  8.55 us
    all_to_all x1, starting transfers between devices, body(): lax.all_to_all(narrowed, 'dp', split_axis=0, concat_axis=1, tiled=True)  7.41 us
  transfers between devices with their start and end apart: 2, of which 2 were waited for; matrix products, arithmetic and copies ran while one was open for 2% of the time, Pallas kernels for 0%

profile of v1, /device:TPU:0, one launch (start us, length us, event | category | flops | bytes accessed | tf_op | source)
XLA Modules:
  0.0 279.6 jit_solution(3642444511742317411)
XLA Ops:
  6.5 5.3 %convert_element_type.32 = bf16[8,128,1792]{2,1,0:T(8,128)(2,1)} convert(f32[8,128,1792]{2,1,0:T(8,128)} %param.2) | non-fusion elementwise | flops 1835008 | bytes 11010048 | tf_op jit(solution)/shard_map/convert_element_type | solution.py:18
  11.9 0.0 copy-start.2
  11.9 7.4 %all-to-all-start = ((bf16[8,128,1792]{2,1,0:T(8,128)(2,1)}), bf16[8,128,1792]{2,1,0:T(8,128)(2,1)}, u32[]{:S(2)}, u32[]{:S(2)}) async-start(bf16[8,128,1792]{2,1,0:T(8,128)(2,1)} %convert_element_type.32), calls=%async_computation | async-start | bytes 7340032 | tf_op jit(solution)/shard_map/all_to_all | solution.py:19
  19.3 0.0 all-reduce.2.cloned.1.call-start
  19.3 0.0 copy-done.2
  19.3 0.6 dynamic_slice.3
  19.9 0.5 iota_compare_fusion.1
  20.5 80.9 %all-to-all-done = bf16[8,128,1792]{2,1,0:T(8,128)(2,1)} async-done(((bf16[8,128,1792]{2,1,0:T(8,128)(2,1)}), bf16[8,128,1792]{2,1,0:T(8,128)(2,1)}, u32[]{:S(2)}, u32[]{:S(2)}) %all-to-all-start) | async-done | bytes 3670048 | tf_op jit(solution)/shard_map/all_to_all | solution.py:19
  101.3 8.6 %convert_bitcast_fusion = bf16[1,1024,1024]{2,1,0:T(8,128)(2,1)} fusion(bf16[1,1024,1,1,1,1,1792]{6,1,5,4,3,2,0:T(8,128)(2,1)} %bitcast.2, pred[1024]{0:T(1024)(128)(4,1)S(1)} %iota_compare_fusion.1), kind=kOutput, calls=%fused_computation.16 | convolution fusion | flops 3760979968 | bytes 5768192 | tf_op jit(solution)/shard_map/mcr,mdr->mcd/dot_general | solution.py:26
  109.9 0.0 all-reduce.2.cloned.1.call-update
  110.5 4.2 %bitcast_select_fusion = bf16[1024,1792]{1,0:T(8,128)(2,1)} fusion(bf16[8,128,1792]{2,1,0:T(8,128)(2,1)} %all-to-all-done, pred[1024]{0:T(1024)(128)(4,1)S(1)} %iota_compare_fusion.1), kind=kLoop, calls=%fused_computation.11 | loop fusion | flops 1835008 | bytes 7341056 | tf_op jit(solution)/shard_map/jit(_where)/select_n | solution.py:25
  114.7 45.9 %all-reduce.2.cloned.1.call-done = bf16[1,1024,1024]{2,1,0:T(8,128)(2,1)} async-done(((bf16[1,1024,1024]{2,1,0:T(8,128)(2,1)}), bf16[1,1024,1024]{2,1,0:T(8,128)(2,1)}) %all-reduce.2.cloned.1.call-update) | async-done | bytes 2097168 | tf_op jit(solution)/shard_map/psum | solution.py:30
  160.5 2.4 fusion
  163.7 0.0 copy-start
  163.7 0.0 copy-start.1
  163.7 9.9 %fusion.2 = f32[1024,1792]{1,0:T(8,128)} fusion(bf16[1,1024,1,1,1,1,1792]{6,1,5,4,3,2,0:T(8,128)(2,1)} %bitcast.2, pred[1024]{0:T(1024)(128)(4,1)S(1)} %iota_compare_fusion.1, bf16[1,1024,1024]{2,1,0:T(8,128)(2,1)} %all-reduce.2.cloned.1.call-done, f32[]{:T(128)} %bitcast.7), kind=kOutput, calls=%fused_computation.7 | convolution fusion | flops 3763077120 | bytes 13108228 | tf_op jit(solution)/shard_map/mcd,mdr->mcr/dot_general | solution.py:36
  173.5 0.0 copy-done
  173.5 0.0 copy-done.1
  173.5 9.9 %fusion.7 = bf16[1,1024,1792]{2,1,0:T(8,128)(2,1)S(1)} fusion(f32[1024,1792]{1,0:T(8,128)} %fusion.2, f32[]{:T(128)} %bitcast.6, f32[]{:T(128)S(6)} %mul.54, bf16[1024,1792]{1,0:T(8,128)(2,1)S(1)} %copy-done, bf16[1,1024,1024]{2,1,0:T(8,128)(2,1)S(1)} %copy-done.1, f32[]{:T(128)} %bitcast.7), kind=kOutput, calls=%fused_computation.14 | convolution fusion | flops 3781427200 | bytes 16777228 | tf_op jit(solution)/shard_map/mcd,mdr->mcr/dot_general | solution.py:39
  183.7 87.2 %all_to_all.20 = bf16[8,1,128,1792]{3,2,1,0:T(8,128)(2,1)S(1)} all-to-all(bf16[8,1,128,1792]{3,2,1,0:T(8,128)(2,1)S(1)} %fusion.11), channel_id=1, replica_groups=mesh['dp'=8,'owner'=4] {'dp'}, dimensions={0} | all-to-all | bytes 7340032 | tf_op jit(solution)/shard_map/all_to_all | solution.py:13
  270.9 1.8 copy.12
  (8 shorter events, 0.3 us)
Async XLA Ops:
  11.9 7.5 %copy-start.2 = (s32[8]{0:T(128)S(1)}, s32[8]{0:T(128)}, u32[]{:S(2)}) copy-start(s32[8]{0:T(128)} %param.3) | copy-start | bytes 100
  11.9 89.5 %all-to-all-start = ((bf16[8,128,1792]{2,1,0:T(8,128)(2,1)}), bf16[8,128,1792]{2,1,0:T(8,128)(2,1)}, u32[]{:S(2)}, u32[]{:S(2)}) async-start(bf16[8,128,1792]{2,1,0:T(8,128)(2,1)} %convert_element_type.32), calls=%async_computation | async-start | bytes 7340032 | tf_op jit(solution)/shard_map/all_to_all | solution.py:19
  19.3 141.2 %all-reduce.2.cloned.1.call-start = ((), (), s32[]{:S(2)}) async-start(), calls=%async_computation.2 | async-start | bytes 4194304 | tf_op jit(solution)/shard_map/psum | solution.py:30
  163.7 9.9 %copy-start = (bf16[1024,1792]{1,0:T(8,128)(2,1)S(1)}, bf16[1024,1792]{1,0:T(8,128)(2,1)}, u32[]{:S(2)}) copy-start(bf16[1024,1792]{1,0:T(8,128)(2,1)} %bitcast_select_fusion) | copy-start | bytes 11010052
  163.7 9.9 %copy-start.1 = (bf16[1,1024,1024]{2,1,0:T(8,128)(2,1)S(1)}, bf16[1,1024,1024]{2,1,0:T(8,128)(2,1)}, u32[]{:S(2)}) copy-start(bf16[1,1024,1024]{2,1,0:T(8,128)(2,1)} %all-reduce.2.cloned.1.call-done) | copy-start | bytes 6291460
Sparse Core Ops, SparseCore 0:
  110.0 50.4 all-reduce.1
